TPU v7x, 32 devices: a whole 2x2x4 slice. The times are simulated.
32 devices in a mesh: dp: 2 (over x), tp: 4 (over z), section: 4 (over y, core).
Axes of the slice: x: 2, y: 2, z: 4, core: 2. Of those that a mesh axis runs over, the one named last changes fastest.
Arguments:
- tokens: bfloat16 [256, 2304], P('dp', 'section'), may hold values from -6 to 6
- hidden_grad: bfloat16 [256, 18432], P('dp', ('tp', 'section')), may hold values from -6 to 6
- norm_gain: float32 [2304], replicated, may hold values from 0.5 to 1.5
- w_gate: bfloat16 [2304, 18432], P('dp', ('tp', 'section')), may hold values from -0.125 to 0.125
- w_up: bfloat16 [2304, 18432], P('dp', ('tp', 'section')), may hold values from -0.125 to 0.125
Outputs:
- grad_tokens: bfloat16 [256, 2304], P('dp', ('tp', 'section'))
- grad_gain: float32 [2304], P(('tp', 'section'))
- grad_gate: bfloat16 [2304, 18432], P('dp', ('tp', 'section'))
- grad_up: bfloat16 [2304, 18432], P('dp', ('tp', 'section'))
All inputs are finite; a program needn't handle non-finite values.
Results may differ from a plain program's by a relative error of at most 0.018.
Values may be sent and summed in bfloat16 or wider, within the bound.
A program may use at most 128 MiB of HBM per device.

v0:
```python
import jax
import jax.numpy as jnp
from jax import lax
from jax.sharding import PartitionSpec as P

D = 2304
epsilon = 1e-06


def gated_unit(gate, up):
    return jax.nn.gelu(gate, approximate=True) * up


def shards(tokens, hidden_grad, norm_gain, w_gate, w_up):
    rows_in = lax.all_gather(tokens, "section", axis=1, tiled=True)
    inputs = rows_in.astype(jnp.float32)
    inv_rms = lax.rsqrt(jnp.mean(inputs * inputs, axis=1) + epsilon)
    normed = (inputs * inv_rms[:, None] * norm_gain).astype(jnp.bfloat16)
    full_gate, full_up = (
        lax.all_gather(w_gate, "dp", axis=0, tiled=True),
        lax.all_gather(w_up, "dp", axis=0, tiled=True),
    )
    gate = jnp.dot(normed, full_gate, preferred_element_type=jnp.float32)
    up = jnp.dot(normed, full_up, preferred_element_type=jnp.float32)
    hidden, pull = jax.vjp(gated_unit, gate, up)
    d_gate, d_up = pull(hidden_grad.astype(jnp.float32))
    d_gate = d_gate.astype(jnp.bfloat16)
    d_up = d_up.astype(jnp.bfloat16)
    contract_cols = (((1,), (1,)), ((), ()))
    contract_rows = (((0,), (0,)), ((), ()))
    features = full_gate.shape[0]
    own_width = features // lax.axis_size(("tp", "section"))
    first = lax.dot_general(full_gate, d_gate, contract_cols, preferred_element_type=jnp.float32)
    second = lax.dot_general(full_up, d_up, contract_cols, preferred_element_type=jnp.float32)
    d_columns = lax.psum_scatter(
        (first + second).astype(jnp.bfloat16), ("tp", "section"), scatter_dimension=0, tiled=True
    ).astype(jnp.float32)
    d_normed = d_columns.T
    offset = lax.axis_index(("tp", "section")) * own_width
    own_inputs = lax.dynamic_slice_in_dim(inputs, offset, own_width, 1)
    own_gain = lax.dynamic_slice_in_dim(norm_gain, offset, own_width, 0)
    gain_part = jnp.sum(d_normed * own_inputs * inv_rms[:, None], axis=0)
    row_part = jnp.sum(own_inputs * own_gain * d_normed, axis=1)
    grad_gain = lax.psum(gain_part, "dp")
    row_sum = lax.psum(row_part, ("tp", "section"))
    grad_tokens = (
        inv_rms[:, None] * own_gain * d_normed - own_inputs * (inv_rms**3 * row_sum / D)[:, None]
    )
    block = w_gate.shape[0]
    fwidth = w_gate.shape[1]
    cols_normed = lax.all_to_all(normed, "dp", split_axis=1, concat_axis=0, tiled=True)
    per_device = normed.shape[0]
    empty = jnp.zeros((block, fwidth), jnp.float32)
    piece_gate = lax.all_gather(d_gate, "dp", axis=0, tiled=True)
    piece_up = lax.all_gather(d_up, "dp", axis=0, tiled=True)

    def one_block(index, running):
        inner = index * per_device
        block_normed = lax.dynamic_slice_in_dim(cols_normed, inner, per_device, 0)
        block_gate = lax.dynamic_slice_in_dim(piece_gate, inner, per_device, 0)
        block_up = lax.dynamic_slice_in_dim(piece_up, inner, per_device, 0)
        terms = (
            lax.dot_general(
                block_normed, block_gate, contract_rows, preferred_element_type=jnp.float32
            ),
            lax.dot_general(
                block_normed, block_up, contract_rows, preferred_element_type=jnp.float32
            ),
        )
        return tuple(
            (
                total + lax.optimization_barrier(term.astype(jnp.bfloat16)).astype(jnp.float32)
                for total, term in zip(running, terms)
            )
        )

    sum_gate, sum_up = lax.fori_loop(
        0, piece_gate.shape[0] // per_device, one_block, (empty, empty)
    )
    return (
        grad_tokens.astype(jnp.bfloat16),
        grad_gain,
        sum_gate.astype(jnp.bfloat16),
        sum_up.astype(jnp.bfloat16),
    )


def solution(mesh):
    in_specs = (
        P("dp", "section"),
        P("dp", ("tp", "section")),
        P(),
        P("dp", ("tp", "section")),
        P("dp", ("tp", "section")),
    )
    out_specs = (
        P("dp", ("tp", "section")),
        P(("tp", "section")),
        P("dp", ("tp", "section")),
        P("dp", ("tp", "section")),
    )
    return jax.shard_map(shards, mesh=mesh, in_specs=in_specs, out_specs=out_specs, check_vma=False)
```

profile of v0, /device:TPU:0, one launch (start us, length us, event | category | flops | bytes accessed | tf_op | source)
XLA Modules:
  0.0 266.3 jit_solution(6498756828406113752)
XLA Ops:
  7.2 0.7 all-gather.5.cloned.1.call-update
  8.0 0.7 all-gather.3.cloned.1.call-update
  8.7 9.0 %all_gather.15 = bf16[128,2304]{0,1:T(8,128)(2,1)S(1)} all-gather(bf16[128,576]{0,1:T(8,128)(2,1)S(1)} %copy-done.3), channel_id=1, replica_groups=mesh['dp'=2,'tp'=4,'section'=4] {'section'}, dimensions={1}, use_global_device_ids=true | all-gather | bytes 737280 | tf_op jit(solution)/shard_map/all_gather | solution.py:15
  17.7 0.3 multiply_reduce_fusion
  18.1 0.4 multiply_convert_fusion
  18.4 1.1 copy.13
  19.5 3.5 %all-to-all-start = ((bf16[128,2,1152]{2,0,1:T(8,128)(2,1)}), bf16[128,2,1152]{2,0,1:T(8,128)(2,1)S(1)}, u32[]{:S(2)}, u32[]{:S(2)}) async-start(bf16[128,2,1152]{2,0,1:T(8,128)(2,1)} %copy.13), calls=%async_computation | async-start | bytes 1179648 | tf_op jit(solution)/shard_map/all_to_all | solution.py:51
  23.1 1.1 convert_element_type.59
  24.3 63.6 %all-gather.5.cloned.1.call-done = bf16[2304,1152]{1,0:T(8,128)(2,1)} async-done(((bf16[1152,1152]{1,0:T(8,128)(2,1)}), bf16[2304,1152]{1,0:T(8,128)(2,1)}) %all-gather.5.cloned.1.call-update) | async-done | bytes 5308432 | tf_op jit(solution)/shard_map/all_gather | solution.py:20
  87.9 3.7 %fusion.8 = (bf16[128,1152]{1,0:T(8,128)(2,1)S(1)}, f32[128,1152]{1,0:T(8,128)S(1)}) fusion(bf16[128,1152]{1,0:T(8,128)(2,1)S(1)} %copy-done.2, bf16[128,2304]{0,1:T(8,128)(2,1)S(1)} %multiply_convert_fusion, bf16[2304,1152]{1,0:T(8,128)(2,1)} %all-gather.5.cloned.1.call-done), kind=kOutput, calls=%fused_computation.19 | convolution fusion | flops 681099264 | bytes 7077888 | tf_op jit(solution)/shard_map/dot_general | solution.py:23
  91.6 67.1 %all-gather.3.cloned.1.call-done = bf16[2304,1152]{1,0:T(8,128)(2,1)} async-done(((bf16[1152,1152]{1,0:T(8,128)(2,1)}), bf16[2304,1152]{1,0:T(8,128)(2,1)}) %all-gather.3.cloned.1.call-update) | async-done | bytes 5308432 | tf_op jit(solution)/shard_map/all_gather | solution.py:21
  158.7 4.0 %fusion.15 = bf16[128,1152]{1,0:T(8,128)(2,1)S(1)} fusion(f32[128,1152]{1,0:T(8,128)S(1)} %get-tuple-element.158, bf16[128,2304]{0,1:T(8,128)(2,1)S(1)} %multiply_convert_fusion, bf16[2304,1152]{1,0:T(8,128)(2,1)} %all-gather.3.cloned.1.call-done, bf16[128,1152]{1,0:T(8,128)(2,1)} %param.8), kind=kOutput, calls=%fused_computation.26 | convolution fusion | flops 682721280 | bytes 7077888 | tf_op jit(solution)/shard_map/dot_general | solution.py:24
  162.7 1.6 fusion.23
  164.3 0.9 copy-done.1
  165.2 1.6 fusion.7
  166.8 1.1 copy.14
  167.9 9.3 %all_gather.19 = bf16[256,1152]{1,0:T(8,128)(2,1)} all-gather(bf16[128,1152]{1,0:T(8,128)(2,1)S(1)} %get-tuple-element.157), channel_id=1, replica_groups=mesh['dp'=2,'tp'=4,'section'=4] {'dp'}, dimensions={0}, use_global_device_ids=true | all-gather | bytes 884736 | tf_op jit(solution)/shard_map/all_gather | solution.py:55
  177.2 8.5 %all_gather.18 = bf16[256,1152]{1,0:T(8,128)(2,1)} all-gather(bf16[128,1152]{1,0:T(8,128)(2,1)S(1)} %fusion.15), channel_id=1, replica_groups=mesh['dp'=2,'tp'=4,'section'=4] {'dp'}, dimensions={0}, use_global_device_ids=true | all-gather | bytes 884736 | tf_op jit(solution)/shard_map/all_gather | solution.py:54
  185.7 27.0 %while.16 = (s32[]{:T(128)}, f32[1152,1152]{1,0:T(8,128)}, f32[1152,1152]{1,0:T(8,128)}, bf16[256,1152]{1,0:T(8,128)(2,1)S(1)}, bf16[256,1152]{1,0:T(8,128)(2,1)...) while((s32[]{:T(128)}, f32[1152,1152]{1,0:T(8,128)}, ...), condition=%wide.region_7.0_spmd.clone, body=%wide.region_6.0_spmd.clone.sunk | while | flops 690094080 | bytes 33032356 | solution.py:77
  185.7 1.8 convolution_convert_fusion.4
  187.6 3.4 %convolution_convert_fusion.5 = bf16[1152,1152]{1,0:T(8,128)(2,1)} fusion(bf16[256,1152]{1,0:T(8,128)(2,1)} %get-tuple-element.224, s32[]{:T(128)S(6)} %select_n.16, bf16[256,1152]{1,0:T(8,128)(2,1)S(1)} %get-tuple-element.223), kind=kOutput, calls=%fused_computation.1.clone.1 | convolution fusion | flops 341065728 | bytes 3245056 | tf_op jit(solution)/shard_map/while/body/eval_jaxpr/dot_general | solution.py:63
  190.9 6.7 %select_add_fusion.3 = (f32[1152,1152]{1,0:T(8,128)}, f32[1152,1152]{1,0:T(8,128)}) fusion(f32[1152,1152]{1,0:T(8,128)} %get-tuple-element.212, bf16[1152,1152]{1,0:T(8,128)(2,1)S(1)} %convolution_convert_fusion.4, pred[]{:T(512)S(6)} %compare.3, bf16[1152,1152]{1,0:T(8,128)(2,1)} %convolution_convert_fusion.5, f32[1152,1152]{1,0:T(8,128)} %get-tuple-element.211), kind=kLoop, calls=%fused_computation.2.clone.1 | loop fusion | flops 7962624 | bytes 26542080 | tf_op jit(solution)/shard_map/while/body/eval_jaxpr/add | solution.py:72
  197.6 1.8 convolution_convert_fusion.4
  199.5 3.4 %convolution_convert_fusion.5 = bf16[1152,1152]{1,0:T(8,128)(2,1)} fusion(bf16[256,1152]{1,0:T(8,128)(2,1)} %get-tuple-element.224, s32[]{:T(128)S(6)} %select_n.16, bf16[256,1152]{1,0:T(8,128)(2,1)S(1)} %get-tuple-element.223), kind=kOutput, calls=%fused_computation.1.clone.1 | convolution fusion | flops 341065728 | bytes 3245056 | tf_op jit(solution)/shard_map/while/body/eval_jaxpr/dot_general | solution.py:63
  202.8 9.9 %select_add_fusion.3 = (f32[1152,1152]{1,0:T(8,128)}, f32[1152,1152]{1,0:T(8,128)}) fusion(f32[1152,1152]{1,0:T(8,128)} %get-tuple-element.212, bf16[1152,1152]{1,0:T(8,128)(2,1)S(1)} %convolution_convert_fusion.4, pred[]{:T(512)S(6)} %compare.3, bf16[1152,1152]{1,0:T(8,128)(2,1)} %convolution_convert_fusion.5, f32[1152,1152]{1,0:T(8,128)} %get-tuple-element.211), kind=kLoop, calls=%fused_computation.2.clone.1 | loop fusion | flops 7962624 | bytes 26542080 | tf_op jit(solution)/shard_map/while/body/eval_jaxpr/add | solution.py:72
  212.7 4.4 %convert_element_type.68 = bf16[1152,1152]{1,0:T(8,128)(2,1)} convert(f32[1152,1152]{1,0:T(8,128)} %get-tuple-element.115) | non-fusion elementwise | flops 1327104 | bytes 7962624 | tf_op jit(solution)/shard_map/convert_element_type | solution.py:84
  217.3 1.8 convert_element_type.67
  219.1 3.0 %reduce-scatter.4.cloned.1.call-done = bf16[144,128]{1,0:T(8,128)(2,1)} async-done(((bf16[2304,128]{1,0:T(8,128)(2,1)}), bf16[144,128]{1,0:T(8,128)(2,1)}) %reduce-scatter.4.cloned.1.call-update) | async-done | bytes 36880 | tf_op jit(solution)/shard_map/reduce_scatter | solution.py:35
  222.1 1.1 fusion.20
  223.2 5.5 %psum.15 = f32[144]{0:T(256)} all-reduce(f32[144]{0:T(256)S(1)} %get-tuple-element.141), channel_id=1, replica_groups=mesh['dp'=2,'tp'=4,'section'=4] {'dp'}, use_global_device_ids=true, to_apply=%region_5.0 | all-reduce | flops 144 | bytes 1152 | tf_op jit(solution)/shard_map/psum | solution.py:44
  228.6 29.5 %psum.14 = f32[128]{0:T(128)S(1)} all-reduce(f32[128]{0:T(128)S(1)} %get-tuple-element.142), channel_id=1, replica_groups=mesh['dp'=2,'tp'=4,'section'=4] {'tp','section'}, use_global_device_ids=true, to_apply=%region_3.0 | all-reduce | flops 128 | bytes 1024 | tf_op jit(solution)/shard_map/psum | solution.py:45
  258.1 1.6 fusion.17
  (24 shorter events, 0.5 us)
Async XLA Ops:
  7.2 1.5 copy-start.3
  7.2 10.9 %copy-start.4 = (f32[2304]{0:T(1024)S(1)}, f32[2304]{0:T(1024)}, u32[]{:S(2)}) copy-start(f32[2304]{0:T(1024)} %param.9) | copy-start | bytes 27652
  7.2 80.7 %all-gather.5.cloned.1.call-start = ((), (), s32[]{:S(2)}) async-start(), calls=%async_computation.3 | async-start | bytes 7962624 | tf_op jit(solution)/shard_map/all_gather | solution.py:20
  7.9 80.0 %copy-start.2 = (bf16[128,1152]{1,0:T(8,128)(2,1)S(1)}, bf16[128,1152]{1,0:T(8,128)(2,1)}, u32[]{:S(2)}) copy-start(bf16[128,1152]{1,0:T(8,128)(2,1)} %param.8) | copy-start | bytes 884740
  7.9 150.8 %all-gather.3.cloned.1.call-start = ((), (), s32[]{:S(2)}) async-start(), calls=%async_computation.2 | async-start | bytes 7962624 | tf_op jit(solution)/shard_map/all_gather | solution.py:21
  19.5 166.2 %all-to-all-start = ((bf16[128,2,1152]{2,0,1:T(8,128)(2,1)}), bf16[128,2,1152]{2,0,1:T(8,128)(2,1)S(1)}, u32[]{:S(2)}, u32[]{:S(2)}) async-start(bf16[128,2,1152]{2,0,1:T(8,128)(2,1)} %copy.13), calls=%async_computation | async-start | bytes 1179648 | tf_op jit(solution)/shard_map/all_to_all | solution.py:51
  23.0 199.1 %reduce-scatter.4.cloned.1.call-start = ((), (), s32[]{:S(2)}) async-start(), calls=%async_computation.4 | async-start | bytes 626688 | tf_op jit(solution)/shard_map/reduce_scatter | solution.py:35
  87.9 74.8 %slice-start = ((s8[5308416]{0:T(1024)(128)(4,1)}), s8[1114112]{0:T(1024)(128)(4,1)S(1)}, s32[]{:S(2)}) async-start(s8[5308416]{0:T(1024)(128)(4,1)} %bitcast.30), calls=%async_computation.5 | async-start | bytes 2228224
  158.7 4.0 %slice-start.1 = ((s8[5308416]{0:T(1024)(128)(4,1)}), s8[4194304]{0:T(1024)(128)(4,1)S(1)}, s32[]{:S(2)}) async-start(s8[5308416]{0:T(1024)(128)(4,1)} %bitcast.30), calls=%async_computation.6 | async-start | bytes 8388608
  162.7 2.5 copy-start.1
  212.7 4.7 %copy-start = (f32[1152,1152]{1,0:T(8,128)S(1)}, f32[1152,1152]{1,0:T(8,128)}, u32[]{:S(2)}) copy-start(f32[1152,1152]{1,0:T(8,128)} %get-tuple-element.114) | copy-start | bytes 15925252
Sparse Core Ops, SparseCore 0:
  9.5 78.3 all-gather.4
  89.4 69.2 all-gather.2
  168.0 54.0 reduce-scatter.3
where the time goes:
time: 267 us; the launch traced here: 266 us
  waiting for transfers between devices  135 us (51%)
  blocking collectives  61.8 us (23%)
  other arithmetic  27.3 us (10%)
  matrix products  21.2 us (8%)
  between operations  13.9 us (5%)
  starting transfers between devices  3.64 us (1%)
  local copies, waits for them, and re-layouts  3.38 us (1%)
    all_gather x1, waiting for transfers between devices, shards(): lax.all_gather(w_up, 'dp', axis=0, tiled=True)  67.1 us
    all_gather x1, waiting for transfers between devices, shards(): lax.all_gather(w_gate, 'dp', axis=0, tiled=True)  63.6 us
    psum x1, blocking collectives, shards(): row_sum = lax.psum(row_part, ('tp', 'section'))  29.5 us
    add x2, other arithmetic, one_block(): total + lax.optimization_barrier(term.astype(jnp.bfloat16)).astype(jnp.fl...  16.6 us
    all_gather x1, blocking collectives, shards(): piece_up = lax.all_gather(d_up, 'dp', axis=0, tiled=True)  9.34 us
    all_gather x1, blocking collectives, shards(): rows_in = lax.all_gather(tokens, 'section', axis=1, tiled=True)  9.03 us
    all_gather x1, blocking collectives, shards(): piece_gate = lax.all_gather(d_gate, 'dp', axis=0, tiled=True)  8.47 us
    dot_general x2, matrix products, one_block(): lax.dot_general(block_normed, block_gate, contract_rows, preferred_elemen...  6.71 us
  transfers between devices with their start and end apart: 4, of which 3 were waited for; matrix products, arithmetic and copies ran while one was open for 18% of the time, Pallas kernels for 0%

commit v1 on v0

--- a/solution.py
+++ b/solution.py
@@ -42,7 +42,9 @@
     gain_part = jnp.sum(d_normed * own_inputs * inv_rms[:, None], axis=0)
     row_part = jnp.sum(own_inputs * own_gain * d_normed, axis=1)
     grad_gain = lax.psum(gain_part, "dp")
-    row_sum = lax.psum(row_part, ("tp", "section"))
+    row_sum = row_part
+    for axis in ("section", "tp"):
+        row_sum = lax.psum(row_sum, axis)
     grad_tokens = (
         inv_rms[:, None] * own_gain * d_normed - own_inputs * (inv_rms**3 * row_sum / D)[:, None]
     )

time: 267 us -> 254 us (0.951)
  blocking collectives: 61.8 us -> 48.9 us
    psum x1 -> x2, blocking collectives: 29.5 us -> 16.6 us  [shards(): row_sum = lax.psum(row_sum, axis)]
  transfers between devices with their start and end apart: 4 -> 4, of which waited for: 3 -> 3; matrix products, arithmetic and copies ran while one was open for 18% -> 19% of each run, Pallas kernels for 0% -> 0%
where the time goes in v1:
time: 254 us; the launch traced here: 253 us
  waiting for transfers between devices  135 us (53%)
  blocking collectives  48.9 us (19%)
  other arithmetic  27.3 us (11%)
  matrix products  21.2 us (8%)
  between operations  13.9 us (5%)
  starting transfers between devices  3.64 us (1%)
  local copies, waits for them, and re-layouts  3.38 us (1%)
    all_gather x1, waiting for transfers between devices, shards(): lax.all_gather(w_up, 'dp', axis=0, tiled=True)  67.1 us
    all_gather x1, waiting for transfers between devices, shards(): lax.all_gather(w_gate, 'dp', axis=0, tiled=True)  63.6 us
    add x2, other arithmetic, one_block(): total + lax.optimization_barrier(term.astype(jnp.bfloat16)).astype(jnp.fl...  16.6 us
    psum x2, blocking collectives, shards(): row_sum = lax.psum(row_sum, axis)  16.6 us
    all_gather x1, blocking collectives, shards(): piece_up = lax.all_gather(d_up, 'dp', axis=0, tiled=True)  9.34 us
    all_gather x1, blocking collectives, shards(): rows_in = lax.all_gather(tokens, 'section', axis=1, tiled=True)  9.03 us
    all_gather x1, blocking collectives, shards(): piece_gate = lax.all_gather(d_gate, 'dp', axis=0, tiled=True)  8.47 us
    dot_general x2, matrix products, one_block(): lax.dot_general(block_normed, block_gate, contract_rows, preferred_elemen...  6.71 us
  transfers between devices with their start and end apart: 4, of which 3 were waited for; matrix products, arithmetic and copies ran while one was open for 19% of the time, Pallas kernels for 0%

profile of v1, /device:TPU:0, one launch (start us, length us, event | category | flops | bytes accessed | tf_op | source)
XLA Modules:
  0.0 253.4 jit_solution(2131282536964239920)
XLA Ops:
  7.2 0.7 all-gather.5.cloned.1.call-update
  8.0 0.7 all-gather.3.cloned.1.call-update
  8.7 9.0 %all_gather.15 = bf16[128,2304]{0,1:T(8,128)(2,1)S(1)} all-gather(bf16[128,576]{0,1:T(8,128)(2,1)S(1)} %copy-done.3), channel_id=1, replica_groups=mesh['dp'=2,'tp'=4,'section'=4] {'section'}, dimensions={1}, use_global_device_ids=true | all-gather | bytes 737280 | tf_op jit(solution)/shard_map/all_gather | solution.py:15
  18.1 0.4 multiply_convert_fusion
  18.4 1.1 copy.13
  19.5 3.5 %all-to-all-start = ((bf16[128,2,1152]{2,0,1:T(8,128)(2,1)}), bf16[128,2,1152]{2,0,1:T(8,128)(2,1)S(1)}, u32[]{:S(2)}, u32[]{:S(2)}) async-start(bf16[128,2,1152]{2,0,1:T(8,128)(2,1)} %copy.13), calls=%async_computation | async-start | bytes 1179648 | tf_op jit(solution)/shard_map/all_to_all | solution.py:53
  23.1 1.1 convert_element_type.59
  24.3 63.6 %all-gather.5.cloned.1.call-done = bf16[2304,1152]{1,0:T(8,128)(2,1)} async-done(((bf16[1152,1152]{1,0:T(8,128)(2,1)}), bf16[2304,1152]{1,0:T(8,128)(2,1)}) %all-gather.5.cloned.1.call-update) | async-done | bytes 5308432 | tf_op jit(solution)/shard_map/all_gather | solution.py:20
  87.9 3.7 %fusion.8 = (bf16[128,1152]{1,0:T(8,128)(2,1)S(1)}, f32[128,1152]{1,0:T(8,128)S(1)}) fusion(bf16[128,1152]{1,0:T(8,128)(2,1)S(1)} %copy-done.2, bf16[128,2304]{0,1:T(8,128)(2,1)S(1)} %multiply_convert_fusion, bf16[2304,1152]{1,0:T(8,128)(2,1)} %all-gather.5.cloned.1.call-done), kind=kOutput, calls=%fused_computation.19 | convolution fusion | flops 681099264 | bytes 7077888 | tf_op jit(solution)/shard_map/dot_general | solution.py:23
  91.6 67.1 %all-gather.3.cloned.1.call-done = bf16[2304,1152]{1,0:T(8,128)(2,1)} async-done(((bf16[1152,1152]{1,0:T(8,128)(2,1)}), bf16[2304,1152]{1,0:T(8,128)(2,1)}) %all-gather.3.cloned.1.call-update) | async-done | bytes 5308432 | tf_op jit(solution)/shard_map/all_gather | solution.py:21
  158.7 4.0 %fusion.15 = bf16[128,1152]{1,0:T(8,128)(2,1)S(1)} fusion(f32[128,1152]{1,0:T(8,128)S(1)} %get-tuple-element.158, bf16[128,2304]{0,1:T(8,128)(2,1)S(1)} %multiply_convert_fusion, bf16[2304,1152]{1,0:T(8,128)(2,1)} %all-gather.3.cloned.1.call-done, bf16[128,1152]{1,0:T(8,128)(2,1)} %param.8), kind=kOutput, calls=%fused_computation.26 | convolution fusion | flops 682721280 | bytes 7077888 | tf_op jit(solution)/shard_map/dot_general | solution.py:24
  162.7 1.6 fusion.23
  164.3 0.9 copy-done.1
  165.2 1.6 fusion.7
  166.8 1.1 copy.14
  167.9 9.3 %all_gather.19 = bf16[256,1152]{1,0:T(8,128)(2,1)} all-gather(bf16[128,1152]{1,0:T(8,128)(2,1)S(1)} %get-tuple-element.157), channel_id=1, replica_groups=mesh['dp'=2,'tp'=4,'section'=4] {'dp'}, dimensions={0}, use_global_device_ids=true | all-gather | bytes 884736 | tf_op jit(solution)/shard_map/all_gather | solution.py:57
  177.2 8.5 %all_gather.18 = bf16[256,1152]{1,0:T(8,128)(2,1)} all-gather(bf16[128,1152]{1,0:T(8,128)(2,1)S(1)} %fusion.15), channel_id=1, replica_groups=mesh['dp'=2,'tp'=4,'section'=4] {'dp'}, dimensions={0}, use_global_device_ids=true | all-gather | bytes 884736 | tf_op jit(solution)/shard_map/all_gather | solution.py:56
  185.7 27.0 %while.16 = (s32[]{:T(128)}, f32[1152,1152]{1,0:T(8,128)}, f32[1152,1152]{1,0:T(8,128)}, bf16[256,1152]{1,0:T(8,128)(2,1)S(1)}, bf16[256,1152]{1,0:T(8,128)(2,1)...) while((s32[]{:T(128)}, f32[1152,1152]{1,0:T(8,128)}, ...), condition=%wide.region_8.0_spmd.clone, body=%wide.region_7.0_spmd.clone.sunk | while | flops 690094080 | bytes 33032356 | solution.py:79
  185.7 1.8 convolution_convert_fusion.4
  187.6 3.4 %convolution_convert_fusion.5 = bf16[1152,1152]{1,0:T(8,128)(2,1)} fusion(bf16[256,1152]{1,0:T(8,128)(2,1)} %get-tuple-element.224, s32[]{:T(128)S(6)} %select_n.16, bf16[256,1152]{1,0:T(8,128)(2,1)S(1)} %get-tuple-element.223), kind=kOutput, calls=%fused_computation.1.clone.1 | convolution fusion | flops 341065728 | bytes 3245056 | tf_op jit(solution)/shard_map/while/body/eval_jaxpr/dot_general | solution.py:65
  190.9 6.7 %select_add_fusion.3 = (f32[1152,1152]{1,0:T(8,128)}, f32[1152,1152]{1,0:T(8,128)}) fusion(f32[1152,1152]{1,0:T(8,128)} %get-tuple-element.212, bf16[1152,1152]{1,0:T(8,128)(2,1)S(1)} %convolution_convert_fusion.4, pred[]{:T(512)S(6)} %compare.3, bf16[1152,1152]{1,0:T(8,128)(2,1)} %convolution_convert_fusion.5, f32[1152,1152]{1,0:T(8,128)} %get-tuple-element.211), kind=kLoop, calls=%fused_computation.2.clone.1 | loop fusion | flops 7962624 | bytes 26542080 | tf_op jit(solution)/shard_map/while/body/eval_jaxpr/add | solution.py:74
  197.6 1.8 convolution_convert_fusion.4
  199.5 3.4 %convolution_convert_fusion.5 = bf16[1152,1152]{1,0:T(8,128)(2,1)} fusion(bf16[256,1152]{1,0:T(8,128)(2,1)} %get-tuple-element.224, s32[]{:T(128)S(6)} %select_n.16, bf16[256,1152]{1,0:T(8,128)(2,1)S(1)} %get-tuple-element.223), kind=kOutput, calls=%fused_computation.1.clone.1 | convolution fusion | flops 341065728 | bytes 3245056 | tf_op jit(solution)/shard_map/while/body/eval_jaxpr/dot_general | solution.py:65
  202.8 9.9 %select_add_fusion.3 = (f32[1152,1152]{1,0:T(8,128)}, f32[1152,1152]{1,0:T(8,128)}) fusion(f32[1152,1152]{1,0:T(8,128)} %get-tuple-element.212, bf16[1152,1152]{1,0:T(8,128)(2,1)S(1)} %convolution_convert_fusion.4, pred[]{:T(512)S(6)} %compare.3, bf16[1152,1152]{1,0:T(8,128)(2,1)} %convolution_convert_fusion.5, f32[1152,1152]{1,0:T(8,128)} %get-tuple-element.211), kind=kLoop, calls=%fused_computation.2.clone.1 | loop fusion | flops 7962624 | bytes 26542080 | tf_op jit(solution)/shard_map/while/body/eval_jaxpr/add | solution.py:74
  212.7 4.4 %convert_element_type.68 = bf16[1152,1152]{1,0:T(8,128)(2,1)} convert(f32[1152,1152]{1,0:T(8,128)} %get-tuple-element.115) | non-fusion elementwise | flops 1327104 | bytes 7962624 | tf_op jit(solution)/shard_map/convert_element_type | solution.py:86
  217.4 1.8 convert_element_type.67
  219.2 2.9 %reduce-scatter.4.cloned.1.call-done = bf16[144,128]{1,0:T(8,128)(2,1)} async-done(((bf16[2304,128]{1,0:T(8,128)(2,1)}), bf16[144,128]{1,0:T(8,128)(2,1)}) %reduce-scatter.4.cloned.1.call-update) | async-done | bytes 36880 | tf_op jit(solution)/shard_map/reduce_scatter | solution.py:35
  222.1 1.1 fusion.20
  223.2 5.5 %psum.23 = f32[144]{0:T(256)} all-reduce(f32[144]{0:T(256)S(1)} %get-tuple-element.141), channel_id=1, replica_groups=mesh['dp'=2,'tp'=4,'section'=4] {'dp'}, use_global_device_ids=true, to_apply=%region_6.0 | all-reduce | flops 144 | bytes 1152 | tf_op jit(solution)/shard_map/psum | solution.py:44
  228.6 5.6 %psum.21 = f32[128]{0:T(128)S(1)} all-reduce(f32[128]{0:T(128)S(1)} %get-tuple-element.142), channel_id=1, replica_groups=mesh['dp'=2,'tp'=4,'section'=4] {'section'}, use_global_device_ids=true, to_apply=%region_3.0 | all-reduce | flops 128 | bytes 1024 | tf_op jit(solution)/shard_map/psum | solution.py:47
  234.3 10.9 %psum.22 = f32[128]{0:T(128)S(1)} all-reduce(f32[128]{0:T(128)S(1)} %psum.21), channel_id=1, replica_groups=mesh['dp'=2,'tp'=4,'section'=4] {'tp'}, use_global_device_ids=true, to_apply=%region_4.0 | all-reduce | flops 128 | bytes 1024 | tf_op jit(solution)/shard_map/psum | solution.py:47
  245.2 1.6 fusion.17
  (25 shorter events, 0.8 us)
Async XLA Ops:
  7.2 1.5 copy-start.3
  7.2 10.9 %copy-start.4 = (f32[2304]{0:T(1024)S(1)}, f32[2304]{0:T(1024)}, u32[]{:S(2)}) copy-start(f32[2304]{0:T(1024)} %param.9) | copy-start | bytes 27652
  7.2 80.7 %all-gather.5.cloned.1.call-start = ((), (), s32[]{:S(2)}) async-start(), calls=%async_computation.3 | async-start | bytes 7962624 | tf_op jit(solution)/shard_map/all_gather | solution.py:20
  7.9 80.0 %copy-start.2 = (bf16[128,1152]{1,0:T(8,128)(2,1)S(1)}, bf16[128,1152]{1,0:T(8,128)(2,1)}, u32[]{:S(2)}) copy-start(bf16[128,1152]{1,0:T(8,128)(2,1)} %param.8) | copy-start | bytes 884740
  7.9 150.8 %all-gather.3.cloned.1.call-start = ((), (), s32[]{:S(2)}) async-start(), calls=%async_computation.2 | async-start | bytes 7962624 | tf_op jit(solution)/shard_map/all_gather | solution.py:21
  19.5 166.2 %all-to-all-start = ((bf16[128,2,1152]{2,0,1:T(8,128)(2,1)}), bf16[128,2,1152]{2,0,1:T(8,128)(2,1)S(1)}, u32[]{:S(2)}, u32[]{:S(2)}) async-start(bf16[128,2,1152]{2,0,1:T(8,128)(2,1)} %copy.13), calls=%async_computation | async-start | bytes 1179648 | tf_op jit(solution)/shard_map/all_to_all | solution.py:53
  23.0 199.1 %reduce-scatter.4.cloned.1.call-start = ((), (), s32[]{:S(2)}) async-start(), calls=%async_computation.4 | async-start | bytes 626688 | tf_op jit(solution)/shard_map/reduce_scatter | solution.py:35
  87.9 74.8 %slice-start = ((s8[5308416]{0:T(1024)(128)(4,1)}), s8[1114112]{0:T(1024)(128)(4,1)S(1)}, s32[]{:S(2)}) async-start(s8[5308416]{0:T(1024)(128)(4,1)} %bitcast.30), calls=%async_computation.5 | async-start | bytes 2228224
  158.7 4.0 %slice-start.1 = ((s8[5308416]{0:T(1024)(128)(4,1)}), s8[4194304]{0:T(1024)(128)(4,1)S(1)}, s32[]{:S(2)}) async-start(s8[5308416]{0:T(1024)(128)(4,1)} %bitcast.30), calls=%async_computation.6 | async-start | bytes 8388608
  162.7 2.5 copy-start.1
  212.7 4.7 %copy-start = (f32[1152,1152]{1,0:T(8,128)S(1)}, f32[1152,1152]{1,0:T(8,128)}, u32[]{:S(2)}) copy-start(f32[1152,1152]{1,0:T(8,128)} %get-tuple-element.114) | copy-start | bytes 15925252
Sparse Core Ops, SparseCore 0:
  9.5 78.3 all-gather.4
  89.4 69.2 all-gather.2
  168.0 54.0 reduce-scatter.3
